TPU v7x, 32 devices: a whole 2x2x4 slice. The times are simulated.
32 devices in a mesh: groups: 2 (over y), rows: 4 (over z), cols: 2 (over x), sub: 2 (over core).
Axes of the slice: x: 2, y: 2, z: 4, core: 2. Of those that a mesh axis runs over, the one named last changes fastest.
Arguments:
- returns: float32 [8, 64, 8192], P('groups', 'rows', ('cols', 'sub')), parts along dimension 0, may hold values from -6 to 6
- starts: int32 [8, 8192], P('groups', ('cols', 'sub')), parts along dimension 0, may hold values from 0 to 32
- start_block: float32 [8, 32, 8192], P('groups', None, ('cols', 'sub')), parts along dimension 0, may hold values from -6 to 6
Outputs:
- loadings: float32 [8, 32, 8192], P('groups', None, ('cols', 'sub')), parts along dimension 0
There are 2 independent parts, one for each index of `groups`. A program takes and returns all parts, laid end to end along the dimension named above; each array names one. Nothing has to cross between parts.
Inputs may be any that keep to these rules, and one draw needn't show every extreme that they name: `starts`: days before an asset's start day hold returns that do not count.
All inputs are finite; a program needn't handle non-finite values.
Results may differ from a plain program's by a relative error of at most 0.0078.
Values may be sent and summed in bfloat16 or wider, within the bound.
A program may use at most 64 MiB of HBM per device.

v0:
```python
import jax
import jax.numpy as jnp
from jax import lax
from jax.sharding import PartitionSpec as P

ASSETS = 8192
ITERS = 3


def gram_of(image):
    return jnp.einsum("wkj,wlj->wkl", image, image, precision=lax.Precision.HIGHEST)


def project(factors, scaled):
    rounded = factors.astype(jnp.bfloat16)
    return jnp.einsum("wka,wta->wkt", rounded, scaled, preferred_element_type=jnp.float32)


def expand(proj, widened):
    return jnp.einsum("wkt,wta->wka", proj, widened, precision=lax.Precision.HIGHEST)


def orthonormal(image, gram):
    lower = jnp.linalg.cholesky(gram / ASSETS)
    return jax.scipy.linalg.solve_triangular(lower, image, lower=True)


def on_device(returns, starts, start_block):
    windows, days, width = returns.shape
    rows_count = lax.axis_size("rows")
    row_pos = lax.axis_index("rows")
    total_days = days * rows_count
    day_index = row_pos * days + jnp.arange(days, dtype=jnp.int32)
    live = (day_index[None, :, None] >= starts[:, None, :]).astype(jnp.float32)
    counts = (total_days - starts).astype(jnp.float32)
    masked = live * returns
    sums = lax.psum(jnp.sum(masked, axis=1), "rows")
    mean = sums / counts
    centered = live * (returns - mean[:, None, :])
    squares = lax.psum(jnp.sum(centered * centered, axis=1), "rows")
    scaled = (centered * lax.rsqrt(squares + 1.0)[:, None, :]).astype(jnp.bfloat16)
    widened = scaled.astype(jnp.float32)
    factors = start_block
    for step in range(ITERS):
        proj = lax.psum(project(factors, scaled), ("cols", "sub"))
        image = lax.psum(expand(proj, widened), "rows")
        gram = lax.psum(gram_of(image), ("cols", "sub"))
        factors = orthonormal(image, gram)
    return factors


def solution(mesh):
    placed = (
        P("groups", "rows", ("cols", "sub")),
        P("groups", ("cols", "sub")),
        P("groups", None, ("cols", "sub")),
    )
    return jax.shard_map(
        on_device,
        mesh=mesh,
        in_specs=placed,
        out_specs=P("groups", None, ("cols", "sub")),
        check_vma=False,
    )
```

profile of v0, /device:TPU:0, one launch (start us, length us, event | category | flops | bytes accessed | tf_op | source)
XLA Modules:
  0.0 354.8 jit_solution(6312155068273593770)
XLA Ops:
  6.5 1.3 fusion
  7.8 0.0 copy-start.4
  7.9 20.9 %psum.77 = f32[4,2048]{1,0:T(4,128)S(1)} all-reduce(f32[4,2048]{1,0:T(4,128)S(1)} %fusion), channel_id=1, replica_groups=mesh['groups'=2,'rows'=4,'cols'=2,'sub'=2] {'rows'}, use_global_device_ids=true, to_apply=%region_1.0 | all-reduce | flops 8192 | bytes 65536 | tf_op jit(solution)/shard_map/psum | solution.py:37
  28.9 0.2 multiply_reduce_fusion
  29.1 15.8 %psum.78 = f32[4,2048]{1,0:T(4,128)S(1)} all-reduce(f32[4,2048]{1,0:T(4,128)S(1)} %multiply_reduce_fusion), channel_id=1, replica_groups=mesh['groups'=2,'rows'=4,'cols'=2,'sub'=2] {'rows'}, use_global_device_ids=true, to_apply=%region_3.0 | all-reduce | flops 8192 | bytes 65536 | tf_op jit(solution)/shard_map/psum | solution.py:40
  44.9 0.2 multiply_convert_fusion
  45.1 0.0 copy-done.4
  45.1 0.2 convolution_bitcast_fusion
  45.3 10.3 %psum.79 = f32[4,32,16]{1,2,0:T(8,128)S(1)} all-reduce(f32[4,32,16]{1,2,0:T(8,128)S(1)} %convolution_bitcast_fusion), channel_id=1, replica_groups=mesh['groups'=2,'rows'=4,'cols'=2,'sub'=2] {'cols','sub'}, use_global_device_ids=true, to_apply=%region_4.0 | all-reduce | flops 2048 | bytes 16384 | tf_op jit(solution)/shard_map/psum | solution.py:45
  55.6 1.6 fusion.9
  57.2 0.0 all-reduce.4.cloned.1.call-update
  57.2 0.0 all-reduce.6.cloned.1.call-start
  57.3 51.6 %all-reduce.4.cloned.1.call-done = f32[4,32,2048]{2,1,0:T(8,128)} async-done(((f32[4,32,2048]{2,1,0:T(8,128)}), f32[4,32,2048]{2,1,0:T(8,128)}) %all-reduce.4.cloned.1.call-update) | async-done | bytes 1048592 | tf_op jit(solution)/shard_map/psum | solution.py:46
  108.8 2.7 fusion.10
  111.6 11.8 %psum.81 = f32[4,32,32]{1,2,0:T(8,128)S(1)} all-reduce(f32[4,32,32]{1,2,0:T(8,128)S(1)} %fusion.10), channel_id=1, replica_groups=mesh['groups'=2,'rows'=4,'cols'=2,'sub'=2] {'cols','sub'}, use_global_device_ids=true, to_apply=%region_6.0 | all-reduce | flops 4096 | bytes 32768 | tf_op jit(solution)/shard_map/psum | solution.py:47
  123.4 0.1 copy.12
  123.6 11.7 %custom-call.10 = f32[4,32,32]{2,1,0:T(8,128)S(1)} custom-call(f32[4,32,32]{2,1,0:T(8,128)S(1)} %fusion.8), custom_call_target="Cholesky" | custom-call | tf_op jit(solution)/shard_map/jit(cholesky)/cholesky | solution.py:24
  135.3 0.1 compare_reduce_fusion.2
  135.4 0.1 select_bitcast_fusion.2
  135.5 9.8 %custom-call.11 = f32[4,1,32,32]{2,3,1,0:T(8,128)S(1)} custom-call(f32[4,1,32,32]{3,2,1,0:T(8,128)S(1)} %select_bitcast_fusion.2), custom_call_target="InvertDiagBlocksLowerTriangular" | custom-call | tf_op jit(solution)/shard_map/jit(_solve_triangular)/vmap()/triangular_solve | solution.py:25
  145.4 1.1 convolution_convert_fusion.1
  146.4 0.2 fusion.11
  146.7 10.5 %psum.82 = f32[4,32,16]{1,2,0:T(8,128)S(1)} all-reduce(f32[4,32,16]{1,2,0:T(8,128)S(1)} %fusion.11), channel_id=1, replica_groups=mesh['groups'=2,'rows'=4,'cols'=2,'sub'=2] {'cols','sub'}, use_global_device_ids=true, to_apply=%region_9.0 | all-reduce | flops 2048 | bytes 16384 | tf_op jit(solution)/shard_map/psum | solution.py:45
  157.2 1.6 fusion.12
  158.8 0.0 all-reduce.6.cloned.1.call-update
  158.8 0.0 all-reduce.8.cloned.1.call-start
  158.8 50.5 %all-reduce.6.cloned.1.call-done = f32[4,32,2048]{2,1,0:T(8,128)} async-done(((f32[4,32,2048]{2,1,0:T(8,128)}), f32[4,32,2048]{2,1,0:T(8,128)}) %all-reduce.6.cloned.1.call-update) | async-done | bytes 1048592 | tf_op jit(solution)/shard_map/psum | solution.py:46
  209.3 2.7 fusion.13
  212.0 11.8 %psum.84 = f32[4,32,32]{1,2,0:T(8,128)S(1)} all-reduce(f32[4,32,32]{1,2,0:T(8,128)S(1)} %fusion.13), channel_id=1, replica_groups=mesh['groups'=2,'rows'=4,'cols'=2,'sub'=2] {'cols','sub'}, use_global_device_ids=true, to_apply=%region_11.0 | all-reduce | flops 4096 | bytes 32768 | tf_op jit(solution)/shard_map/psum | solution.py:47
  223.9 0.1 copy.14
  224.0 11.7 %custom-call.12 = f32[4,32,32]{2,1,0:T(8,128)S(1)} custom-call(f32[4,32,32]{2,1,0:T(8,128)S(1)} %fusion.6), custom_call_target="Cholesky" | custom-call | tf_op jit(solution)/shard_map/jit(cholesky)/cholesky | solution.py:24
  235.8 0.1 compare_reduce_fusion.1
  235.9 0.1 select_bitcast_fusion.1
  236.0 9.8 %custom-call.13 = f32[4,1,32,32]{2,3,1,0:T(8,128)S(1)} custom-call(f32[4,1,32,32]{3,2,1,0:T(8,128)S(1)} %select_bitcast_fusion.1), custom_call_target="InvertDiagBlocksLowerTriangular" | custom-call | tf_op jit(solution)/shard_map/jit(_solve_triangular)/vmap()/triangular_solve | solution.py:25
  245.8 1.1 convolution_convert_fusion
  246.9 0.2 fusion.14
  247.1 10.5 %psum.85 = f32[4,32,16]{1,2,0:T(8,128)S(1)} all-reduce(f32[4,32,16]{1,2,0:T(8,128)S(1)} %fusion.14), channel_id=1, replica_groups=mesh['groups'=2,'rows'=4,'cols'=2,'sub'=2] {'cols','sub'}, use_global_device_ids=true, to_apply=%region_12.0 | all-reduce | flops 2048 | bytes 16384 | tf_op jit(solution)/shard_map/psum | solution.py:45
  257.6 1.6 fusion.15
  259.2 0.0 all-reduce.8.cloned.1.call-update
  259.2 50.5 %all-reduce.8.cloned.1.call-done = f32[4,32,2048]{2,1,0:T(8,128)} async-done(((f32[4,32,2048]{2,1,0:T(8,128)}), f32[4,32,2048]{2,1,0:T(8,128)}) %all-reduce.8.cloned.1.call-update) | async-done | bytes 1048592 | tf_op jit(solution)/shard_map/psum | solution.py:46
  309.7 2.7 fusion.16
  312.5 11.8 %psum.87 = f32[4,32,32]{1,2,0:T(8,128)S(1)} all-reduce(f32[4,32,32]{1,2,0:T(8,128)S(1)} %fusion.16), channel_id=1, replica_groups=mesh['groups'=2,'rows'=4,'cols'=2,'sub'=2] {'cols','sub'}, use_global_device_ids=true, to_apply=%region_14.17 | all-reduce | flops 4096 | bytes 32768 | tf_op jit(solution)/shard_map/psum | solution.py:47
  324.4 0.1 copy.16
  324.5 11.7 %custom-call.14 = f32[4,32,32]{2,1,0:T(8,128)S(1)} custom-call(f32[4,32,32]{2,1,0:T(8,128)S(1)} %fusion.4), custom_call_target="Cholesky" | custom-call | tf_op jit(solution)/shard_map/jit(cholesky)/cholesky | solution.py:24
  336.2 0.1 compare_reduce_fusion
  336.3 0.1 select_bitcast_fusion
  336.4 9.8 %custom-call.15 = f32[4,1,32,32]{2,3,1,0:T(8,128)S(1)} custom-call(f32[4,1,32,32]{3,2,1,0:T(8,128)S(1)} %select_bitcast_fusion), custom_call_target="InvertDiagBlocksLowerTriangular" | custom-call | tf_op jit(solution)/shard_map/jit(_solve_triangular)/vmap()/triangular_solve | solution.py:25
  346.3 2.0 fusion.2
  (25 shorter events, 0.2 us)
Async XLA Ops:
  6.5 22.3 %copy-start.3 = (f32[4,16,2048]{2,1,0:T(8,128)S(1)}, f32[4,16,2048]{2,1,0:T(8,128)}, u32[]{:S(2)}) copy-start(f32[4,16,2048]{2,1,0:T(8,128)} %param.6) | copy-start | bytes 1572868
  6.5 102.3 %all-reduce.4.cloned.1.call-start = ((), (), s32[]{:S(2)}) async-start(), calls=%async_computation | async-start | bytes 2097152 | tf_op jit(solution)/shard_map/psum | solution.py:46
  6.5 22.3 %copy-start.5 = (s32[4,2048]{1,0:T(4,128)S(1)}, s32[4,2048]{1,0:T(4,128)}, u32[]{:S(2)}) copy-start(s32[4,2048]{1,0:T(4,128)} %param.7) | copy-start | bytes 98308
  7.8 37.2 %copy-start.4 = (f32[4,32,2048]{2,1,0:T(8,128)S(1)}, f32[4,32,2048]{2,1,0:T(8,128)}, u32[]{:S(2)}) copy-start(f32[4,32,2048]{2,1,0:T(8,128)} %param.8) | copy-start | bytes 3145732
  57.2 152.1 %all-reduce.6.cloned.1.call-start = ((), (), s32[]{:S(2)}) async-start(), calls=%async_computation.1 | async-start | bytes 2097152 | tf_op jit(solution)/shard_map/psum | solution.py:46
  108.8 36.5 %copy-start = (f32[4,32,2048]{2,1,0:T(8,128)S(1)}, f32[4,32,2048]{2,1,0:T(8,128)}, u32[]{:S(2)}) copy-start(f32[4,32,2048]{2,1,0:T(8,128)} %all-reduce.4.cloned.1.call-done) | copy-start | bytes 3145732
  158.8 151.0 %all-reduce.8.cloned.1.call-start = ((), (), s32[]{:S(2)}) async-start(), calls=%async_computation.2 | async-start | bytes 2097152 | tf_op jit(solution)/shard_map/psum | solution.py:46
  209.3 36.5 %copy-start.1 = (f32[4,32,2048]{2,1,0:T(8,128)S(1)}, f32[4,32,2048]{2,1,0:T(8,128)}, u32[]{:S(2)}) copy-start(f32[4,32,2048]{2,1,0:T(8,128)} %all-reduce.6.cloned.1.call-done) | copy-start | bytes 3145732
  309.7 36.5 %copy-start.2 = (f32[4,32,2048]{2,1,0:T(8,128)S(1)}, f32[4,32,2048]{2,1,0:T(8,128)}, u32[]{:S(2)}) copy-start(f32[4,32,2048]{2,1,0:T(8,128)} %all-reduce.8.cloned.1.call-done) | copy-start | bytes 3145732
Sparse Core Ops, SparseCore 0:
  57.3 51.4 all-reduce.3
  158.9 50.3 all-reduce.5
  259.3 50.3 all-reduce.7
where the time goes:
time: 355 us
  waiting for transfers between devices  153 us (43%)
  blocking collectives  103 us (29%)
  other arithmetic  67.2 us (19%)
  matrix products  17.9 us (5%)
  between operations  13.4 us (4%)
    psum x3, waiting for transfers between devices, on_device(): image = lax.psum(expand(proj, widened), 'rows')  153 us
    another operation x10, other arithmetic, orthonormal(): lower = jnp.linalg.cholesky(gram / ASSETS)  35.6 us
    psum x3, blocking collectives, on_device(): gram = lax.psum(gram_of(image), ('cols', 'sub'))  35.5 us
    psum x3, blocking collectives, on_device(): proj = lax.psum(project(factors, scaled), ('cols', 'sub'))  31.2 us
    another operation x7, other arithmetic, orthonormal(): return jax.scipy.linalg.solve_triangular(lower, image, lower=True)  29.8 us
    psum x1, blocking collectives, on_device(): sums = lax.psum(jnp.sum(masked, axis=1), 'rows')  20.9 us
    psum x1, blocking collectives, on_device(): squares = lax.psum(jnp.sum(centered * centered, axis=1), 'rows')  15.8 us
    dot_general x3, matrix products, gram_of(): jnp.einsum('wkj,wlj->wkl', image, image, precision=lax.Precision.HIGHEST)  8.19 us
  transfers between devices with their start and end apart: 3, of which 3 were waited for; matrix products, arithmetic and copies ran while one was open for 0% of the time, Pallas kernels for 0%

commit v1 on v0

v1 whole, which is shorter than its diff:
```python
import functools

import jax
import jax.numpy as jnp
from jax import lax
from jax.experimental import pallas as pl
from jax.experimental.pallas import tpu as pltpu
from jax.sharding import PartitionSpec as P

ITERS = 3
HIGHEST = lax.Precision.HIGHEST
MESH = pl.DeviceIdType.MESH
NT = (((1,), (1,)), ((), ()))
SUBLANES = 8


def eliminate(gram, right):
    size = gram.shape[0]
    height = min(SUBLANES, size)
    blocks = size // height
    gs = [gram[b * height:(b + 1) * height] for b in range(blocks)]
    rs = [right[b * height:(b + 1) * height] for b in range(blocks)]
    row_id = lax.broadcasted_iota(jnp.int32, (height, 1), 0)
    diag = [jnp.ones((height, 1), jnp.float32) for _ in range(blocks)]
    for j in range(size):
        b, i = divmod(j, height)
        grow = gs[b][i:i + 1]
        rrow = rs[b][i:i + 1]
        pivot = gs[b][i:i + 1, j:j + 1]
        diag[b] = jnp.where(row_id == i, pivot, diag[b])
        inverse = 1.0 / pivot
        for c in range(b, blocks):
            factor = gs[c][:, j:j + 1] * inverse
            if c == b:
                factor = jnp.where(row_id > i, factor, 0.0)
            gs[c] = gs[c] - factor * grow
            rs[c] = rs[c] - factor * rrow
    return jnp.concatenate([r * lax.rsqrt(d) for r, d in zip(rs, diag)], axis=0)


def kernel(rows, cols, subs, assets,
           returns_ref, starts_ref, start_ref, out_ref,
           xbuf, sbuf, part, rs, mine, quad, mloc, mall,
           xs, xr, ss, sr, ps, pr, qs, qr, ms, mr):
    r = lax.axis_index("rows")
    mates = cols * subs
    m = lax.axis_index("cols") * subs + lax.axis_index("sub")
    windows, days, width = returns_ref.shape
    k = start_ref.shape[1]
    total = days * rows
    own = width // rows

    def row_peer(d):
        return lax.rem(r + d, rows)

    def mate(d):
        return lax.rem(m + d, mates)

    def row_id(q):
        return {"rows": q}

    def mate_id(q):
        return {"cols": q // subs, "sub": lax.rem(q, subs)}

    def columns(q):
        return pl.ds(pl.multiple_of(q * own, own), own)

    barrier = pltpu.get_barrier_semaphore()
    for d in range(1, rows):
        pl.semaphore_signal(barrier, inc=1, device_id=row_id(row_peer(d)), device_id_type=MESH)
    for d in range(1, mates):
        pl.semaphore_signal(barrier, inc=1, device_id=mate_id(mate(d)), device_id_type=MESH)
    pl.semaphore_wait(barrier, rows - 1 + mates - 1)

    def copy_to(src, dst, send, recv, target):
        return pltpu.make_async_remote_copy(
            src_ref=src, dst_ref=dst, send_sem=send, recv_sem=recv,
            device_id=target, device_id_type=MESH)

    sends = []
    for w in range(windows):
        for d in range(1, rows):
            q = row_peer(d)
            c = copy_to(returns_ref.at[w, :, columns(q)], xbuf.at[r, w], xs.at[w, d],
                        xr.at[w, r], row_id(q))
            c.start()
            sends.append(c)
    xbuf[r] = returns_ref[:, :, columns(r)]

    day = lax.broadcasted_iota(jnp.int32, (total, own), 0)
    for w in range(windows):
        for d in range(1, rows):
            q = row_peer(d)
            copy_to(returns_ref.at[w, :, columns(q)], xbuf.at[q, w], xs.at[w, d],
                    xr.at[w, q], row_id(q)).wait_recv()
        x = jnp.concatenate([xbuf[q, w] for q in range(rows)], axis=0)
        begin = starts_ref[pl.ds(w, 1), columns(r)]
        live = day >= begin
        counts = (total - begin).astype(jnp.float32)
        mean = jnp.sum(jnp.where(live, x, 0.0), axis=0, keepdims=True) / counts
        centered = jnp.where(live, x - mean, 0.0)
        squares = jnp.sum(centered * centered, axis=0, keepdims=True)
        scaled = (centered * lax.rsqrt(squares + 1.0)).astype(jnp.bfloat16)
        sbuf[r, w] = scaled
        first = start_ref[w, :, columns(r)].astype(jnp.bfloat16)
        part[w] = lax.dot_general(jnp.concatenate([first, scaled], axis=0), scaled, NT,
                                  preferred_element_type=jnp.float32)

    for d in range(1, rows):
        q = row_peer(d)
        c = copy_to(part.at[q], rs.at[r], ps.at[d], pr.at[r], row_id(q))
        c.start()
        sends.append(c)
    for d in range(1, rows):
        q = row_peer(d)
        c = copy_to(sbuf.at[r], sbuf.at[r], ss.at[d], sr.at[r], row_id(q))
        c.start()
        sends.append(c)
    rs[r] = part[r]
    for d in range(1, rows):
        q = row_peer(d)
        copy_to(part.at[q], rs.at[q], ps.at[d], pr.at[q], row_id(q)).wait_recv()
    summed = rs[0]
    for q in range(1, rows):
        summed = summed + rs[q]
    mine[...] = summed
    for d in range(1, mates):
        q = mate(d)
        c = copy_to(mine, quad.at[m], qs.at[d], qr.at[m], mate_id(q))
        c.start()
        sends.append(c)
    quad[m] = summed
    for d in range(1, mates):
        q = mate(d)
        copy_to(mine, quad.at[q], qs.at[d], qr.at[q], mate_id(q)).wait_recv()
    both = quad[0]
    for q in range(1, mates):
        both = both + quad[q]
    proj, corr = both[:k], both[k:]
    for step in range(ITERS):
        image = jnp.dot(proj, corr, precision=HIGHEST, preferred_element_type=jnp.float32)
        gram = lax.dot_general(image, proj, NT, precision=HIGHEST,
                               preferred_element_type=jnp.float32) / assets
        proj = eliminate(gram, image if step < ITERS - 1 else proj)
    mloc[...] = proj
    for d in range(1, rows):
        q = row_peer(d)
        c = copy_to(mloc, mall.at[r], ms.at[d], mr.at[r], row_id(q))
        c.start()
        sends.append(c)
    mall[r] = proj
    for d in range(1, rows):
        q = row_peer(d)
        copy_to(mloc, mall.at[q], ms.at[d], mr.at[q], row_id(q)).wait_recv()
    stacked = []
    for w in range(windows):
        value = mall[w]
        high = value.astype(jnp.bfloat16)
        low = (value - high.astype(jnp.float32)).astype(jnp.bfloat16)
        stacked.append(jnp.concatenate([high, low], axis=0))

    def finish(q):
        for w in range(windows):
            wide = jnp.dot(stacked[w], sbuf[q, w], preferred_element_type=jnp.float32)
            out_ref[w, :, columns(q)] = wide[:k] + wide[k:]

    finish(r)
    for d in range(1, rows):
        q = row_peer(d)
        copy_to(sbuf.at[q], sbuf.at[q], ss.at[d], sr.at[q], row_id(q)).wait_recv()
        finish(q)
    for c in sends:
        c.wait_send()


def fused(returns, starts, start_block, rows, cols, subs):
    windows, days, width = returns.shape
    k = start_block.shape[1]
    total = days * rows
    own = width // rows
    mates = cols * subs
    f32 = jnp.float32
    dma = pltpu.SemaphoreType.DMA
    return pl.pallas_call(
        functools.partial(kernel, rows, cols, subs, width * mates),
        out_shape=jax.ShapeDtypeStruct(start_block.shape, f32),
        in_specs=[pl.BlockSpec(memory_space=pltpu.VMEM)] * 3,
        out_specs=pl.BlockSpec(memory_space=pltpu.VMEM),
        scratch_shapes=[
            pltpu.VMEM((rows, windows, days, own), f32),
            pltpu.VMEM((rows, windows, total, own), jnp.bfloat16),
            pltpu.VMEM((windows, k + total, total), f32),
            pltpu.VMEM((rows, k + total, total), f32),
            pltpu.VMEM((k + total, total), f32),
            pltpu.VMEM((mates, k + total, total), f32),
            pltpu.VMEM((k, total), f32),
            pltpu.VMEM((windows, k, total), f32),
            dma((windows, rows)), dma((windows, rows)),
            dma((rows,)), dma((rows,)),
            dma((rows,)), dma((rows,)),
            dma((mates,)), dma((mates,)),
            dma((rows,)), dma((rows,)),
        ],
        compiler_params=pltpu.CompilerParams(collective_id=0, has_side_effects=True),
    )(returns, starts, start_block)


def gram_of(image):
    return jnp.einsum("wkj,wlj->wkl", image, image, precision=HIGHEST)


def project(factors, scaled):
    rounded = factors.astype(jnp.bfloat16)
    return jnp.einsum("wka,wta->wkt", rounded, scaled, preferred_element_type=jnp.float32)


def expand(proj, widened):
    return jnp.einsum("wkt,wta->wka", proj, widened, precision=HIGHEST)


def orthonormal(image, gram, assets):
    lower = jnp.linalg.cholesky(gram / assets)
    return jax.scipy.linalg.solve_triangular(lower, image, lower=True)


def stepwise(returns, starts, start_block, rows, mates):
    windows, days, width = returns.shape
    row_pos = lax.axis_index("rows")
    total_days = days * rows
    day_index = row_pos * days + jnp.arange(days, dtype=jnp.int32)
    live = (day_index[None, :, None] >= starts[:, None, :]).astype(jnp.float32)
    counts = (total_days - starts).astype(jnp.float32)
    masked = live * returns
    sums = lax.psum(jnp.sum(masked, axis=1), "rows")
    mean = sums / counts
    centered = live * (returns - mean[:, None, :])
    squares = lax.psum(jnp.sum(centered * centered, axis=1), "rows")
    scaled = (centered * lax.rsqrt(squares + 1.0)[:, None, :]).astype(jnp.bfloat16)
    widened = scaled.astype(jnp.float32)
    factors = start_block
    for step in range(ITERS):
        proj = lax.psum(project(factors, scaled), ("cols", "sub"))
        image = lax.psum(expand(proj, widened), "rows")
        gram = lax.psum(gram_of(image), ("cols", "sub"))
        factors = orthonormal(image, gram, width * mates)
    return factors


def on_device(rows, cols, subs, returns, starts, start_block):
    windows, days, width = returns.shape
    k = start_block.shape[1]
    fits = (windows == rows and width % (128 * rows) == 0 and days % 8 == 0 and k % 16 == 0
            and days * rows <= 128 and rows > 1 and cols * subs > 1)
    if fits:
        return fused(returns, starts, start_block, rows, cols, subs)
    return stepwise(returns, starts, start_block, rows, cols * subs)


def solution(mesh):
    placed = (
        P("groups", "rows", ("cols", "sub")),
        P("groups", ("cols", "sub")),
        P("groups", None, ("cols", "sub")),
    )
    sizes = (mesh.shape["rows"], mesh.shape["cols"], mesh.shape["sub"])
    return jax.shard_map(
        functools.partial(on_device, *sizes),
        mesh=mesh,
        in_specs=placed,
        out_specs=P("groups", None, ("cols", "sub")),
        check_vma=False,
    )
```

time: 355 us -> 55.1 us (0.16)
  waiting for transfers between devices: 153 us -> 0 us
  blocking collectives: 103 us -> 0 us
  other arithmetic: 67.2 us -> 0 us
  Pallas kernels: 0 us -> 52.7 us
  matrix products: 17.9 us -> 0 us
  between operations: 13.4 us -> 0.01 us
    psum x3 -> x0, waiting for transfers between devices: 153 us -> none  [on_device(): image = lax.psum(expand(proj, widened), 'rows')]
    psum x8 -> x0, blocking collectives: 103 us -> none  [the longest x3 35.5 us: on_device(): gram = lax.psum(gram_of(image), ('cols', 'sub'))]
    another operation x17 -> x0, other arithmetic: 65.4 us -> none  [the longest x10 35.6 us: orthonormal(): lower = jnp.linalg.cholesky(gram / ASSETS)]
    pallas_call x0 -> x1, Pallas kernels: none -> 52.7 us  [fused(): pl.pallas_call(functools.partial(kernel, rows, cols, subs, width * mates)...]
    dot_general x9 -> x0, matrix products: 13.7 us -> none  [the longest x3 8.19 us: gram_of(): jnp.einsum('wkj,wlj->wkl', image, image, precision=lax.Precision.HIGHEST)]
    another operation x3 -> x0, matrix products: 4.19 us -> none  [orthonormal(): return jax.scipy.linalg.solve_triangular(lower, image, lower=True)]
  transfers between devices with their start and end apart: 3 -> 0, of which waited for: 3 -> 0; matrix products, arithmetic and copies ran while one was open for 0% -> 0% of each run, Pallas kernels for 0% -> 0%
where the time goes in v1:
time: 55.1 us; the launch traced here: 55 us
  Pallas kernels  52.7 us (96%)
  local copies, waits for them, and re-layouts  2.3 us (4%)
    pallas_call x1, Pallas kernels, fused(): pl.pallas_call(functools.partial(kernel, rows, cols, subs, width * mates)...  52.7 us
    unnamed x1, local copies, waits for them, and re-layouts  2.3 us

profile of v1, /device:TPU:0, one launch (start us, length us, event | category | flops | bytes accessed | tf_op | source)
XLA Modules:
  0.0 55.0 jit_solution(6879112092715077549)
XLA Ops:
  0.0 52.7 %shard_map.37 = f32[4,32,2048]{2,1,0:T(8,128)} custom-call(f32[4,16,2048]{2,1,0:T(8,128)} %returns_ref.1, s32[4,2048]{1,0:T(4,128)} %starts_ref.1, f32[4,32,2048]{2,1,0:T(8,128)} %start_ref.1), custom_call_target="tpu_custom_call" | custom-call | tf_op jit(solution)/shard_map/pallas_call | solution.py:184
  52.7 2.3 %copy.5 = f32[4,32,2048]{2,1,0:T(8,128)} copy(f32[4,32,2048]{2,1,0:T(8,128)} %shard_map.37) | data formatting | bytes 2097152

commit v2 on v1

--- a/solution.py
+++ b/solution.py
@@ -40,8 +40,8 @@
 
 def kernel(rows, cols, subs, assets,
            returns_ref, starts_ref, start_ref, out_ref,
-           xbuf, sbuf, part, rs, mine, quad, mloc, mall,
-           xs, xr, ss, sr, ps, pr, qs, qr, ms, mr):
+           held, begins, firsts, obuf, xbuf, sbuf, part, rs, mine, quad, mloc, mall,
+           ls, bs, os, xs, xr, to_right, to_left, sr, ps, pr, qs, qr, ms, mr):
     r = lax.axis_index("rows")
     mates = cols * subs
     m = lax.axis_index("cols") * subs + lax.axis_index("sub")
@@ -49,6 +49,7 @@
     k = start_ref.shape[1]
     total = days * rows
     own = width // rows
+    half = (k + total) // 2
 
     def row_peer(d):
         return lax.rem(r + d, rows)
@@ -64,6 +65,14 @@
 
     def columns(q):
         return pl.ds(pl.multiple_of(q * own, own), own)
+
+    loads = [pltpu.make_async_copy(returns_ref.at[w], held.at[w], ls.at[w]) for w in range(windows)]
+    for c in loads:
+        c.start()
+    load_begins = pltpu.make_async_copy(starts_ref.at[:, columns(r)], begins, bs.at[0])
+    load_begins.start()
+    load_firsts = pltpu.make_async_copy(start_ref.at[:, :, columns(r)], firsts, bs.at[1])
+    load_firsts.start()
 
     barrier = pltpu.get_barrier_semaphore()
     for d in range(1, rows):
@@ -79,22 +88,25 @@
 
     sends = []
     for w in range(windows):
+        loads[w].wait()
         for d in range(1, rows):
             q = row_peer(d)
-            c = copy_to(returns_ref.at[w, :, columns(q)], xbuf.at[r, w], xs.at[w, d],
+            c = copy_to(held.at[w, :, columns(q)], xbuf.at[r, w], xs.at[w, d],
                         xr.at[w, r], row_id(q))
             c.start()
             sends.append(c)
-    xbuf[r] = returns_ref[:, :, columns(r)]
+    xbuf[r] = held[:, :, columns(r)]
+    load_begins.wait()
+    load_firsts.wait()
 
     day = lax.broadcasted_iota(jnp.int32, (total, own), 0)
     for w in range(windows):
         for d in range(1, rows):
             q = row_peer(d)
-            copy_to(returns_ref.at[w, :, columns(q)], xbuf.at[q, w], xs.at[w, d],
+            copy_to(held.at[w, :, columns(q)], xbuf.at[q, w], xs.at[w, d],
                     xr.at[w, q], row_id(q)).wait_recv()
         x = jnp.concatenate([xbuf[q, w] for q in range(rows)], axis=0)
-        begin = starts_ref[pl.ds(w, 1), columns(r)]
+        begin = begins[w:w + 1]
         live = day >= begin
         counts = (total - begin).astype(jnp.float32)
         mean = jnp.sum(jnp.where(live, x, 0.0), axis=0, keepdims=True) / counts
@@ -102,24 +114,54 @@
         squares = jnp.sum(centered * centered, axis=0, keepdims=True)
         scaled = (centered * lax.rsqrt(squares + 1.0)).astype(jnp.bfloat16)
         sbuf[r, w] = scaled
-        first = start_ref[w, :, columns(r)].astype(jnp.bfloat16)
-        part[w] = lax.dot_general(jnp.concatenate([first, scaled], axis=0), scaled, NT,
-                                  preferred_element_type=jnp.float32)
+        first = firsts[w].astype(jnp.bfloat16)
+        sums = lax.dot_general(jnp.concatenate([first, scaled], axis=0), scaled, NT,
+                               preferred_element_type=jnp.float32)
+        part[w] = jnp.concatenate([sums[:half], sums[half:]], axis=1)
 
     for d in range(1, rows):
         q = row_peer(d)
         c = copy_to(part.at[q], rs.at[r], ps.at[d], pr.at[r], row_id(q))
         c.start()
         sends.append(c)
-    for d in range(1, rows):
-        q = row_peer(d)
-        c = copy_to(sbuf.at[r], sbuf.at[r], ss.at[d], sr.at[r], row_id(q))
-        c.start()
-        sends.append(c)
+
+    def hop(q, w, right):
+        sem = to_right if right else to_left
+        target = row_id(lax.rem(r + (1 if right else rows - 1), rows))
+        return copy_to(sbuf.at[q, w], sbuf.at[q, w], sem.at[q, w], sr.at[q, w], target)
+
+    def hops(t, some, act):
+        right_block = lax.rem(r - t + rows, rows)
+        left_block = lax.rem(r + t, rows)
+        for w in some:
+            @pl.when(jnp.logical_and(r - t >= 0, r < rows - 1))
+            def _():
+                act(hop(right_block, w, True), t > 0)
+
+            @pl.when(jnp.logical_and(r + t < rows, r > 0))
+            def _():
+                act(hop(left_block, w, False), t > 0)
+
+    def forward(t, some):
+        for w in some:
+            if t > 0:
+                @pl.when(r - t >= 0)
+                def _():
+                    hop(lax.rem(r - t + rows, rows), w, True).wait_recv()
+
+                @pl.when(r + t < rows)
+                def _():
+                    hop(lax.rem(r + t, rows), w, True).wait_recv()
+            hops(t, (w,), lambda c, _: c.start())
+
+    early, late = range(windows // 2), range(windows // 2, windows)
+    schedule = [(t, some) for t in range(1, rows) for some in (early, late)]
+    forward(0, range(windows))
     rs[r] = part[r]
     for d in range(1, rows):
         q = row_peer(d)
         copy_to(part.at[q], rs.at[q], ps.at[d], pr.at[q], row_id(q)).wait_recv()
+    forward(*schedule.pop(0))
     summed = rs[0]
     for q in range(1, rows):
         summed = summed + rs[q]
@@ -133,11 +175,15 @@
     for d in range(1, mates):
         q = mate(d)
         copy_to(mine, quad.at[q], qs.at[d], qr.at[q], mate_id(q)).wait_recv()
+    forward(*schedule.pop(0))
     both = quad[0]
     for q in range(1, mates):
         both = both + quad[q]
+    both = jnp.concatenate([both[:, :total], both[:, total:]], axis=0)
     proj, corr = both[:k], both[k:]
     for step in range(ITERS):
+        if step > 0 and len(schedule) > 2:
+            forward(*schedule.pop(0))
         image = jnp.dot(proj, corr, precision=HIGHEST, preferred_element_type=jnp.float32)
         gram = lax.dot_general(image, proj, NT, precision=HIGHEST,
                                preferred_element_type=jnp.float32) / assets
@@ -149,6 +195,8 @@
         c.start()
         sends.append(c)
     mall[r] = proj
+    for entry in schedule:
+        forward(*entry)
     for d in range(1, rows):
         q = row_peer(d)
         copy_to(mloc, mall.at[q], ms.at[d], mr.at[q], row_id(q)).wait_recv()
@@ -162,15 +210,23 @@
     def finish(q):
         for w in range(windows):
             wide = jnp.dot(stacked[w], sbuf[q, w], preferred_element_type=jnp.float32)
-            out_ref[w, :, columns(q)] = wide[:k] + wide[k:]
+            obuf[q, w] = wide[:k] + wide[k:]
+        c = pltpu.make_async_copy(obuf.at[q], out_ref.at[:, :, columns(q)], os.at[q])
+        c.start()
 
     finish(r)
-    for d in range(1, rows):
-        q = row_peer(d)
-        copy_to(sbuf.at[q], sbuf.at[q], ss.at[d], sr.at[q], row_id(q)).wait_recv()
-        finish(q)
+    for t in range(1, rows):
+        for near in (True, False):
+            @pl.when(r - t >= 0 if near else r + t < rows)
+            def _():
+                q = lax.rem(r - t + rows if near else r + t, rows)
+                finish(q)
     for c in sends:
         c.wait_send()
+    for t in range(rows):
+        hops(t, range(windows), lambda c, _: c.wait_send())
+    for q in range(rows):
+        pltpu.make_async_copy(obuf.at[q], out_ref.at[:, :, columns(q)], os.at[q]).wait()
 
 
 def fused(returns, starts, start_block, rows, cols, subs):
@@ -179,24 +235,30 @@
     total = days * rows
     own = width // rows
     mates = cols * subs
+    half = (k + total) // 2
     f32 = jnp.float32
     dma = pltpu.SemaphoreType.DMA
     return pl.pallas_call(
         functools.partial(kernel, rows, cols, subs, width * mates),
         out_shape=jax.ShapeDtypeStruct(start_block.shape, f32),
-        in_specs=[pl.BlockSpec(memory_space=pltpu.VMEM)] * 3,
-        out_specs=pl.BlockSpec(memory_space=pltpu.VMEM),
+        in_specs=[pl.BlockSpec(memory_space=pl.ANY)] * 3,
+        out_specs=pl.BlockSpec(memory_space=pl.ANY),
         scratch_shapes=[
+            pltpu.VMEM(returns.shape, f32),
+            pltpu.VMEM((windows, own), jnp.int32),
+            pltpu.VMEM((windows, k, own), f32),
+            pltpu.VMEM((rows, windows, k, own), f32),
             pltpu.VMEM((rows, windows, days, own), f32),
             pltpu.VMEM((rows, windows, total, own), jnp.bfloat16),
-            pltpu.VMEM((windows, k + total, total), f32),
-            pltpu.VMEM((rows, k + total, total), f32),
-            pltpu.VMEM((k + total, total), f32),
-            pltpu.VMEM((mates, k + total, total), f32),
+            pltpu.VMEM((windows, half, 2 * total), f32),
+            pltpu.VMEM((rows, half, 2 * total), f32),
+            pltpu.VMEM((half, 2 * total), f32),
+            pltpu.VMEM((mates, half, 2 * total), f32),
             pltpu.VMEM((k, total), f32),
             pltpu.VMEM((windows, k, total), f32),
+            dma((windows,)), dma((2,)), dma((rows,)),
             dma((windows, rows)), dma((windows, rows)),
-            dma((rows,)), dma((rows,)),
+            dma((rows, windows)), dma((rows, windows)), dma((rows, windows)),
             dma((rows,)), dma((rows,)),
             dma((mates,)), dma((mates,)),
             dma((rows,)), dma((rows,)),
@@ -250,7 +312,7 @@
     windows, days, width = returns.shape
     k = start_block.shape[1]
     fits = (windows == rows and width % (128 * rows) == 0 and days % 8 == 0 and k % 16 == 0
-            and days * rows <= 128 and rows > 1 and cols * subs > 1)
+            and days * rows <= 64 and (days * rows + k) % 16 == 0 and rows > 1 and cols * subs > 1)
     if fits:
         return fused(returns, starts, start_block, rows, cols, subs)
     return stepwise(returns, starts, start_block, rows, cols * subs)

time: 55.1 us -> 45.9 us (0.83)
  Pallas kernels: 52.7 us -> 43.4 us
    pallas_call x1, Pallas kernels: 52.7 us -> 43.4 us  [fused(): pl.pallas_call(functools.partial(kernel, rows, cols, subs, width * mates)...]
where the time goes in v2:
time: 45.9 us; the launch traced here: 45.7 us
  Pallas kernels  43.4 us (95%)
  local copies, waits for them, and re-layouts  2.3 us (5%)
    pallas_call x1, Pallas kernels, fused(): pl.pallas_call(functools.partial(kernel, rows, cols, subs, width * mates)...  43.4 us
    unnamed x1, local copies, waits for them, and re-layouts  2.3 us

profile of v2, /device:TPU:0, one launch (start us, length us, event | category | flops | bytes accessed | tf_op | source)
XLA Modules:
  0.0 45.7 jit_solution(15982626831238624717)
XLA Ops:
  0.0 43.4 %shard_map.37 = f32[4,32,2048]{2,1,0:T(8,128)} custom-call(f32[4,16,2048]{2,1,0:T(8,128)} %returns_ref.1, s32[4,2048]{1,0:T(4,128)} %starts_ref.1, f32[4,32,2048]{2,1,0:T(8,128)} %start_ref.1), custom_call_target="tpu_custom_call" | custom-call | tf_op jit(solution)/shard_map/pallas_call | solution.py:241
  43.4 2.3 %copy.5 = f32[4,32,2048]{2,1,0:T(8,128)} copy(f32[4,32,2048]{2,1,0:T(8,128)} %shard_map.37) | data formatting | bytes 2097152

commit v3 on v2

--- a/solution.py
+++ b/solution.py
@@ -99,6 +99,39 @@
     load_begins.wait()
     load_firsts.wait()
 
+    def hop(q, w, right):
+        sem = to_right if right else to_left
+        target = row_id(lax.rem(r + (1 if right else rows - 1), rows))
+        return copy_to(sbuf.at[q, w], sbuf.at[q, w], sem.at[q, w], sr.at[q, w], target)
+
+    def hops(t, some, act):
+        right_block = lax.rem(r - t + rows, rows)
+        left_block = lax.rem(r + t, rows)
+        for w in some:
+            @pl.when(jnp.logical_and(r - t >= 0, r < rows - 1))
+            def _():
+                act(hop(right_block, w, True), t > 0)
+
+            @pl.when(jnp.logical_and(r + t < rows, r > 0))
+            def _():
+                act(hop(left_block, w, False), t > 0)
+
+    def forward(t, some):
+        for w in some:
+            if t > 0:
+                @pl.when(r - t >= 0)
+                def _():
+                    hop(lax.rem(r - t + rows, rows), w, True).wait_recv()
+
+                @pl.when(r + t < rows)
+                def _():
+                    hop(lax.rem(r + t, rows), w, True).wait_recv()
+            hops(t, (w,), lambda c, _: c.start())
+
+    def deliver(w):
+        return copy_to(part.at[w], rs.at[r], ps.at[w], pr.at[r], row_id(w))
+
+    ahead = windows // 2
     day = lax.broadcasted_iota(jnp.int32, (total, own), 0)
     for w in range(windows):
         for d in range(1, rows):
@@ -119,48 +152,21 @@
                                preferred_element_type=jnp.float32)
         part[w] = jnp.concatenate([sums[:half], sums[half:]], axis=1)
 
-    for d in range(1, rows):
-        q = row_peer(d)
-        c = copy_to(part.at[q], rs.at[r], ps.at[d], pr.at[r], row_id(q))
-        c.start()
-        sends.append(c)
-
-    def hop(q, w, right):
-        sem = to_right if right else to_left
-        target = row_id(lax.rem(r + (1 if right else rows - 1), rows))
-        return copy_to(sbuf.at[q, w], sbuf.at[q, w], sem.at[q, w], sr.at[q, w], target)
-
-    def hops(t, some, act):
-        right_block = lax.rem(r - t + rows, rows)
-        left_block = lax.rem(r + t, rows)
-        for w in some:
-            @pl.when(jnp.logical_and(r - t >= 0, r < rows - 1))
-            def _():
-                act(hop(right_block, w, True), t > 0)
-
-            @pl.when(jnp.logical_and(r + t < rows, r > 0))
-            def _():
-                act(hop(left_block, w, False), t > 0)
-
-    def forward(t, some):
-        for w in some:
-            if t > 0:
-                @pl.when(r - t >= 0)
-                def _():
-                    hop(lax.rem(r - t + rows, rows), w, True).wait_recv()
-
-                @pl.when(r + t < rows)
-                def _():
-                    hop(lax.rem(r + t, rows), w, True).wait_recv()
-            hops(t, (w,), lambda c, _: c.start())
+        @pl.when(r != w)
+        def _():
+            deliver(w).start()
+
+        if w < ahead:
+            forward(0, (w,))
+
 
     early, late = range(windows // 2), range(windows // 2, windows)
     schedule = [(t, some) for t in range(1, rows) for some in (early, late)]
-    forward(0, range(windows))
+    forward(0, range(ahead, windows))
     rs[r] = part[r]
     for d in range(1, rows):
         q = row_peer(d)
-        copy_to(part.at[q], rs.at[q], ps.at[d], pr.at[q], row_id(q)).wait_recv()
+        copy_to(part.at[q], rs.at[q], ps.at[q], pr.at[q], row_id(q)).wait_recv()
     forward(*schedule.pop(0))
     summed = rs[0]
     for q in range(1, rows):
@@ -223,6 +229,10 @@
                 finish(q)
     for c in sends:
         c.wait_send()
+    for w in range(windows):
+        @pl.when(r != w)
+        def _():
+            deliver(w).wait_send()
     for t in range(rows):
         hops(t, range(windows), lambda c, _: c.wait_send())
     for q in range(rows):

time: 45.9 us -> 44.7 us (0.974)
  Pallas kernels: 43.4 us -> 42.2 us
    pallas_call x1, Pallas kernels: 43.4 us -> 42.2 us  [fused(): pl.pallas_call(functools.partial(kernel, rows, cols, subs, width * mates)...]
where the time goes in v3:
time: 44.7 us; the launch traced here: 44.5 us
  Pallas kernels  42.2 us (94%)
  local copies, waits for them, and re-layouts  2.3 us (5%)
    pallas_call x1, Pallas kernels, fused(): pl.pallas_call(functools.partial(kernel, rows, cols, subs, width * mates)...  42.2 us
    unnamed x1, local copies, waits for them, and re-layouts  2.3 us

profile of v3, /device:TPU:0, one launch (start us, length us, event | category | flops | bytes accessed | tf_op | source)
XLA Modules:
  0.0 44.5 jit_solution(7508525626502375505)
XLA Ops:
  0.0 42.2 %shard_map.37 = f32[4,32,2048]{2,1,0:T(8,128)} custom-call(f32[4,16,2048]{2,1,0:T(8,128)} %returns_ref.1, s32[4,2048]{1,0:T(4,128)} %starts_ref.1, f32[4,32,2048]{2,1,0:T(8,128)} %start_ref.1), custom_call_target="tpu_custom_call" | custom-call | tf_op jit(solution)/shard_map/pallas_call | solution.py:251
  42.2 2.3 %copy.5 = f32[4,32,2048]{2,1,0:T(8,128)} copy(f32[4,32,2048]{2,1,0:T(8,128)} %shard_map.37) | data formatting | bytes 2097152

commit v4 on v3

--- a/solution.py
+++ b/solution.py
@@ -21,20 +21,28 @@
     gs = [gram[b * height:(b + 1) * height] for b in range(blocks)]
     rs = [right[b * height:(b + 1) * height] for b in range(blocks)]
     row_id = lax.broadcasted_iota(jnp.int32, (height, 1), 0)
-    diag = [jnp.ones((height, 1), jnp.float32) for _ in range(blocks)]
-    for j in range(size):
-        b, i = divmod(j, height)
-        grow = gs[b][i:i + 1]
-        rrow = rs[b][i:i + 1]
-        pivot = gs[b][i:i + 1, j:j + 1]
-        diag[b] = jnp.where(row_id == i, pivot, diag[b])
-        inverse = 1.0 / pivot
-        for c in range(b, blocks):
-            factor = gs[c][:, j:j + 1] * inverse
-            if c == b:
-                factor = jnp.where(row_id > i, factor, 0.0)
-            gs[c] = gs[c] - factor * grow
-            rs[c] = rs[c] - factor * rrow
+    diag = [jnp.ones((height, right.shape[1]), jnp.float32) for _ in range(blocks)]
+    wide = max(size, right.shape[1])
+    for b in range(blocks):
+        panel = {
+            (c, i): jnp.broadcast_to(gs[c][:, b * height + i:b * height + i + 1], (height, wide))
+            for c in range(b, blocks) for i in range(height)
+        }
+        for i in range(height):
+            grow = gs[b][i:i + 1]
+            rrow = rs[b][i:i + 1]
+            pivot = panel[b, i][i:i + 1]
+            diag[b] = jnp.where(row_id == i, pivot[:, :right.shape[1]], diag[b])
+            inverse = 1.0 / pivot
+            ahead = {n: panel[b, n][i:i + 1] for n in range(i + 1, height)}
+            for c in range(b, blocks):
+                factor = panel[c, i] * inverse
+                if c == b:
+                    factor = jnp.where(row_id > i, factor, 0.0)
+                for n in range(i + 1, height):
+                    panel[c, n] = panel[c, n] - factor * ahead[n]
+                gs[c] = gs[c] - factor[:, :size] * grow
+                rs[c] = rs[c] - factor[:, :right.shape[1]] * rrow
     return jnp.concatenate([r * lax.rsqrt(d) for r, d in zip(rs, diag)], axis=0)
 
 

time: 44.7 us -> 42.5 us (0.951)
  Pallas kernels: 42.2 us -> 40 us
    pallas_call x1, Pallas kernels: 42.2 us -> 40 us  [fused(): pl.pallas_call(functools.partial(kernel, rows, cols, subs, width * mates)...]
where the time goes in v4:
time: 42.5 us; the launch traced here: 42.3 us
  Pallas kernels  40 us (94%)
  local copies, waits for them, and re-layouts  2.3 us (5%)
    pallas_call x1, Pallas kernels, fused(): pl.pallas_call(functools.partial(kernel, rows, cols, subs, width * mates)...  40 us
    unnamed x1, local copies, waits for them, and re-layouts  2.3 us

profile of v4, /device:TPU:0, one launch (start us, length us, event | category | flops | bytes accessed | tf_op | source)
XLA Modules:
  0.0 42.3 jit_solution(4762233954004428896)
XLA Ops:
  0.0 40.0 %shard_map.37 = f32[4,32,2048]{2,1,0:T(8,128)} custom-call(f32[4,16,2048]{2,1,0:T(8,128)} %returns_ref.1, s32[4,2048]{1,0:T(4,128)} %starts_ref.1, f32[4,32,2048]{2,1,0:T(8,128)} %start_ref.1), custom_call_target="tpu_custom_call" | custom-call | tf_op jit(solution)/shard_map/pallas_call | solution.py:259
  40.1 2.3 %copy.5 = f32[4,32,2048]{2,1,0:T(8,128)} copy(f32[4,32,2048]{2,1,0:T(8,128)} %shard_map.37) | data formatting | bytes 2097152
